TPU v7x, 32 devices: a whole 2x2x4 slice. The times are simulated.
32 devices in a mesh: depth: 2 (over x), row: 4 (over y, core), col: 4 (over z).
Axes of the slice: x: 2, y: 2, z: 4, core: 2. Of those that a mesh axis runs over, the one named last changes fastest.
Arguments:
- q_slab: float32 [1536, 1024], P('col', ('depth', 'row')), may hold values from -6 to 6
- triangle: float32 [1024, 1024], P(None, 'depth'), as said below
- panel_q: float32 [32768, 1024], P('row', ('depth', 'col')), may hold values from -0.1875 to 0.1875
Outputs:
- slab_out: float32 [1536, 32768], P('col', 'row')
Inputs may be any that keep to these rules, and one draw needn't show every extreme that they name: triangle is zero below its diagonal; its diagonal lies in 0.5 to 1.5.
All inputs are finite; a program needn't handle non-finite values.
Results may differ from a plain program's by a relative error of at most 0.000071.
Values sent between devices are 32-bit elements; how exact they have to be, the bound alone decides.
A program may use at most 64 MiB of HBM per device.

v0:
```python
import jax
import jax.numpy as jnp
from jax import lax
from jax.sharding import PartitionSpec as P


def per_device(q_slab, triangle, panel_q):
    rows = q_slab.shape[0]
    width = triangle.shape[1]
    share = width // lax.axis_size("row")
    factor = lax.dynamic_slice_in_dim(triangle, lax.axis_index("row") * share, share, 1)
    left = jnp.dot(
        lax.all_gather(q_slab, ("depth", "row"), axis=1, tiled=True),
        factor,
        precision=lax.Precision.HIGHEST,
        preferred_element_type=jnp.float32,
    )
    left = lax.all_gather(left, "row", axis=1, tiled=True)
    narrow = panel_q.shape[1]
    columns = lax.axis_size("col")
    mixed = lax.all_to_all(panel_q, "depth", split_axis=0, concat_axis=1, tiled=True)
    left_all = lax.all_gather(left, "depth", axis=1, tiled=True)
    grid = left_all.reshape(rows, 2, columns, narrow)
    piece = lax.all_gather(mixed, "col", axis=1, tiled=True)
    count = piece.shape[1] // (2 * narrow)
    pieces = piece.reshape(piece.shape[0], count, 2, narrow)
    partial_out = jnp.einsum(
        "sdnw,rndw->sr",
        grid,
        pieces,
        precision=lax.Precision.HIGHEST,
        preferred_element_type=jnp.float32,
    )
    return lax.all_gather(partial_out, "depth", axis=1, tiled=True)


def solution(mesh):
    placed = (P("col", ("depth", "row")), P(None, "depth"), P("row", ("depth", "col")))
    return jax.shard_map(
        per_device, mesh=mesh, in_specs=placed, out_specs=P("col", "row"), check_vma=False
    )
```

profile of v0, /device:TPU:0, one launch (start us, length us, event | category | flops | bytes accessed | tf_op | source)
XLA Modules:
  0.0 567.0 jit_solution(8736152346896375355)
XLA Ops:
  6.5 0.0 copy-start
  6.5 0.0 all-gather.5.cloned.1.call-start
  6.5 0.7 all-gather.5.cloned.1.call-update
  7.3 5.6 all-to-all-start
  12.9 0.0 all-gather.7.cloned.1.call-start
  12.9 31.0 %all-gather.5.cloned.1.call-done = f32[384,1024]{1,0:T(8,128)} async-done(((f32[384,128]{1,0:T(8,128)}), f32[384,1024]{1,0:T(8,128)}) %all-gather.5.cloned.1.call-update) | async-done | bytes 1572880 | tf_op jit(solution)/shard_map/all_gather | solution.py:13
  44.0 0.0 copy-done
  44.0 3.3 convolution_bitcast_fusion
  47.3 9.1 %all_gather.16 = f32[384,512]{0,1:T(8,128)} all-gather(f32[384,128]{0,1:T(8,128)S(1)} %convolution_bitcast_fusion), channel_id=1, replica_groups=mesh['depth'=2,'row'=4,'col'=4] {'row'}, dimensions={1}, use_global_device_ids=true | all-gather | bytes 983040 | tf_op jit(solution)/shard_map/all_gather | solution.py:18
  56.4 0.0 all-gather.7.cloned.1.call-update
  56.4 0.0 all-gather.9.cloned.1.call-start
  56.5 13.7 %all-to-all-done = f32[2,4096,128]{2,1,0:T(8,128)} async-done(((f32[2,4096,128]{2,1,0:T(8,128)}), f32[2,4096,128]{2,1,0:T(8,128)}, u32[]{:S(2)}, u32[]{:S(2)}) %all-to-all-start) | async-done | bytes 4194336 | tf_op jit(solution)/shard_map/all_to_all | solution.py:21
  70.2 5.6 copy.7
  75.8 0.0 all-gather.9.cloned.1.call-update
  75.8 0.0 all-gather.11.cloned.1.call-start
  75.8 9.2 %all-gather.7.cloned.1.call-done = f32[384,1024]{0,1:T(8,128)} async-done(((f32[384,512]{0,1:T(8,128)}), f32[384,1024]{0,1:T(8,128)}) %all-gather.7.cloned.1.call-update) | async-done | bytes 1572880 | tf_op jit(solution)/shard_map/all_gather | solution.py:22
  85.1 288.9 %all-gather.9.cloned.1.call-done = f32[4096,1024]{0,1:T(8,128)} async-done(((f32[4096,256]{0,1:T(8,128)}), f32[4096,1024]{0,1:T(8,128)}) %all-gather.9.cloned.1.call-update) | async-done | bytes 16777232 | tf_op jit(solution)/shard_map/all_gather | solution.py:24
  374.0 24.7 %fusion.2 = f32[384,4096]{1,0:T(8,128)} fusion(f32[384,2,4,128]{0,3,2,1:T(8,128)} %bitcast.16, f32[4096,4,2,128]{0,3,2,1:T(8,128)} %bitcast.13), kind=kOutput, calls=%fused_computation.2 | convolution fusion | flops 19327352832 | bytes 24641536 | tf_op jit(solution)/shard_map/sdnw,rndw->sr/dot_general | solution.py:27
  398.7 0.0 all-gather.11.cloned.1.call-update
  398.7 150.8 %all-gather.11.cloned.1.call-done = f32[384,8192]{1,0:T(8,128)} async-done(((f32[384,4096]{1,0:T(8,128)}), f32[384,8192]{1,0:T(8,128)}) %all-gather.11.cloned.1.call-update) | async-done | bytes 12582928 | tf_op jit(solution)/shard_map/all_gather | solution.py:34
  549.6 0.0 copy-start.1
  549.6 10.9 %copy.19 = f32[384,8192]{1,0:T(8,128)} copy(f32[384,8192]{1,0:T(8,128)} %all-gather.11.cloned.1.call-done) | data formatting | bytes 25165824
  560.5 0.0 copy-done.1
Async XLA Ops:
  6.5 37.4 %copy-start = (f32[1024,512]{1,0:T(8,128)S(1)}, f32[1024,512]{1,0:T(8,128)}, u32[]{:S(2)}) copy-start(f32[1024,512]{1,0:T(8,128)} %param.4) | copy-start | bytes 6291460
  6.5 37.4 %all-gather.5.cloned.1.call-start = ((), (), s32[]{:S(2)}) async-start(), calls=%async_computation.1 | async-start | bytes 1769472 | tf_op jit(solution)/shard_map/all_gather | solution.py:13
  7.3 62.9 %all-to-all-start = ((f32[2,4096,128]{2,1,0:T(8,128)}), f32[2,4096,128]{2,1,0:T(8,128)}, u32[]{:S(2)}, u32[]{:S(2)}) async-start(f32[2,4096,128]{2,1,0:T(8,128)} %bitcast.15), calls=%async_computation | async-start | bytes 8388608 | tf_op jit(solution)/shard_map/all_to_all | solution.py:21
  12.9 72.2 %all-gather.7.cloned.1.call-start = ((), (), s32[]{:S(2)}) async-start(), calls=%async_computation.2 | async-start | bytes 2359296 | tf_op jit(solution)/shard_map/all_gather | solution.py:22
  56.4 317.6 %all-gather.9.cloned.1.call-start = ((), (), s32[]{:S(2)}) async-start(), calls=%async_computation.3 | async-start | bytes 20971520 | tf_op jit(solution)/shard_map/all_gather | solution.py:24
  75.8 473.8 %all-gather.11.cloned.1.call-start = ((), (), s32[]{:S(2)}) async-start(), calls=%async_computation.4 | async-start | bytes 18874368 | tf_op jit(solution)/shard_map/all_gather | solution.py:34
  549.6 10.9 %copy-start.1 = (f32[1024,512]{1,0:T(8,128)S(1)}, f32[1024,512]{1,0:T(8,128)}, u32[]{:S(2)}) copy-start(f32[1024,512]{1,0:T(8,128)} %param.4) | copy-start | bytes 6291460
Sparse Core Ops, SparseCore 0:
  9.2 34.7 all-gather.4
  56.6 28.4 all-gather.6
  86.6 287.3 all-gather.8
  398.8 150.6 all-gather.10
where the time goes:
time: 567 us
  waiting for transfers between devices  494 us (87%)
  matrix products  28 us (5%)
  local copies, waits for them, and re-layouts  16.5 us (3%)
  between operations  13.1 us (2%)
  blocking collectives  9.12 us (2%)
  starting transfers between devices  5.74 us (1%)
    all_gather x1, waiting for transfers between devices, per_device(): piece = lax.all_gather(mixed, 'col', axis=1, tiled=True)  289 us
    all_gather x1, waiting for transfers between devices, per_device(): return lax.all_gather(partial_out, 'depth', axis=1, tiled=True)  151 us
    all_gather x1, waiting for transfers between devices, per_device(): lax.all_gather(q_slab, ('depth', 'row'), axis=1, tiled=True)  31 us
    dot_general x1, matrix products, per_device(): jnp.einsum('sdnw,rndw->sr', grid, pieces, precision=lax.Precision.HIGHEST...  24.7 us
    all_to_all x1, waiting for transfers between devices, per_device(): lax.all_to_all(panel_q, 'depth', split_axis=0, concat_axis=1, tiled=True)  13.7 us
  transfers between devices with their start and end apart: 5, of which 5 were waited for; matrix products, arithmetic and copies ran while one was open for 2% of the time, Pallas kernels for 0%

commit v1 on v0

--- a/solution.py
+++ b/solution.py
@@ -31,7 +31,7 @@
         precision=lax.Precision.HIGHEST,
         preferred_element_type=jnp.float32,
     )
-    return lax.all_gather(partial_out, "depth", axis=1, tiled=True)
+    return jnp.concatenate(lax.all_gather(partial_out, "depth"), axis=1)
 
 
 def solution(mesh):

time: 567 us -> 567 us (level)
    reshape x0 -> x1, local copies, waits for them, and re-layouts: none -> 11.1 us  [per_device(): return jnp.concatenate(lax.all_gather(partial_out, 'depth'), axis=1)]
    unnamed x5 -> x4, local copies, waits for them, and re-layouts: 10.9 us -> 0.01 us
where the time goes in v1:
time: 567 us
  waiting for transfers between devices  494 us (87%)
  matrix products  28 us (5%)
  local copies, waits for them, and re-layouts  16.7 us (3%)
  between operations  13.1 us (2%)
  blocking collectives  9.12 us (2%)
  starting transfers between devices  5.74 us (1%)
    all_gather x1, waiting for transfers between devices, per_device(): piece = lax.all_gather(mixed, 'col', axis=1, tiled=True)  289 us
    all_gather x1, waiting for transfers between devices, per_device(): return jnp.concatenate(lax.all_gather(partial_out, 'depth'), axis=1)  151 us
    all_gather x1, waiting for transfers between devices, per_device(): lax.all_gather(q_slab, ('depth', 'row'), axis=1, tiled=True)  31 us
    dot_general x1, matrix products, per_device(): jnp.einsum('sdnw,rndw->sr', grid, pieces, precision=lax.Precision.HIGHEST...  24.7 us
    all_to_all x1, waiting for transfers between devices, per_device(): lax.all_to_all(panel_q, 'depth', split_axis=0, concat_axis=1, tiled=True)  13.7 us
  transfers between devices with their start and end apart: 5, of which 5 were waited for; matrix products, arithmetic and copies ran while one was open for 2% of the time, Pallas kernels for 0%

profile of v1, /device:TPU:0, one launch (start us, length us, event | category | flops | bytes accessed | tf_op | source)
XLA Modules:
  0.0 567.2 jit_solution(2484230032205384579)
XLA Ops:
  6.5 0.0 copy-start
  6.5 0.0 all-gather.6.cloned.1.call-start
  6.5 0.7 all-gather.6.cloned.1.call-update
  7.3 5.6 all-to-all-start
  12.9 0.0 all-gather.8.cloned.1.call-start
  12.9 31.0 %all-gather.6.cloned.1.call-done = f32[384,1024]{1,0:T(8,128)} async-done(((f32[384,128]{1,0:T(8,128)}), f32[384,1024]{1,0:T(8,128)}) %all-gather.6.cloned.1.call-update) | async-done | bytes 1572880 | tf_op jit(solution)/shard_map/all_gather | solution.py:13
  44.0 0.0 copy-done
  44.0 3.3 convolution_bitcast_fusion
  47.3 9.1 %all_gather.19 = f32[384,512]{0,1:T(8,128)} all-gather(f32[384,128]{0,1:T(8,128)S(1)} %convolution_bitcast_fusion), channel_id=1, replica_groups=mesh['depth'=2,'row'=4,'col'=4] {'row'}, dimensions={1}, use_global_device_ids=true | all-gather | bytes 983040 | tf_op jit(solution)/shard_map/all_gather | solution.py:18
  56.4 0.0 all-gather.8.cloned.1.call-update
  56.4 0.0 all-gather.10.cloned.1.call-start
  56.5 13.7 %all-to-all-done = f32[2,4096,128]{2,1,0:T(8,128)} async-done(((f32[2,4096,128]{2,1,0:T(8,128)}), f32[2,4096,128]{2,1,0:T(8,128)}, u32[]{:S(2)}, u32[]{:S(2)}) %all-to-all-start) | async-done | bytes 4194336 | tf_op jit(solution)/shard_map/all_to_all | solution.py:21
  70.2 5.6 copy.9
  75.8 0.0 all-gather.10.cloned.1.call-update
  75.8 0.0 all-gather.12.cloned.1.call-start
  75.8 9.2 %all-gather.8.cloned.1.call-done = f32[384,1024]{0,1:T(8,128)} async-done(((f32[384,512]{0,1:T(8,128)}), f32[384,1024]{0,1:T(8,128)}) %all-gather.8.cloned.1.call-update) | async-done | bytes 1572880 | tf_op jit(solution)/shard_map/all_gather | solution.py:22
  85.1 288.9 %all-gather.10.cloned.1.call-done = f32[4096,1024]{0,1:T(8,128)} async-done(((f32[4096,256]{0,1:T(8,128)}), f32[4096,1024]{0,1:T(8,128)}) %all-gather.10.cloned.1.call-update) | async-done | bytes 16777232 | tf_op jit(solution)/shard_map/all_gather | solution.py:24
  374.0 24.7 %fusion.2 = f32[384,4096]{1,0:T(8,128)} fusion(f32[384,2,4,128]{0,3,2,1:T(8,128)} %bitcast.22, f32[4096,4,2,128]{0,3,2,1:T(8,128)} %bitcast.18), kind=kOutput, calls=%fused_computation.2 | convolution fusion | flops 19327352832 | bytes 24641536 | tf_op jit(solution)/shard_map/sdnw,rndw->sr/dot_general | solution.py:27
  398.7 0.0 all-gather.12.cloned.1.call-update
  398.7 150.8 %all-gather.12.cloned.1.call-done = f32[768,4096]{1,0:T(8,128)} async-done(((f32[384,4096]{1,0:T(8,128)}), f32[768,4096]{1,0:T(8,128)}) %all-gather.12.cloned.1.call-update) | async-done | bytes 12582928 | tf_op jit(solution)/shard_map/all_gather | solution.py:34
  549.6 0.0 copy-start.1
  549.6 11.1 %copy.17 = f32[2,48,8,4096]{3,2,0,1:T(8,128)} copy(f32[2,48,8,4096]{3,2,1,0:T(8,128)} %bitcast.20) | data formatting | bytes 25165824 | tf_op jit(solution)/shard_map/reshape | solution.py:34
  560.6 0.0 copy-done.1
Async XLA Ops:
  6.5 37.4 %copy-start = (f32[1024,512]{1,0:T(8,128)S(1)}, f32[1024,512]{1,0:T(8,128)}, u32[]{:S(2)}) copy-start(f32[1024,512]{1,0:T(8,128)} %param.4) | copy-start | bytes 6291460
  6.5 37.4 %all-gather.6.cloned.1.call-start = ((), (), s32[]{:S(2)}) async-start(), calls=%async_computation.1 | async-start | bytes 1769472 | tf_op jit(solution)/shard_map/all_gather | solution.py:13
  7.3 62.9 %all-to-all-start = ((f32[2,4096,128]{2,1,0:T(8,128)}), f32[2,4096,128]{2,1,0:T(8,128)}, u32[]{:S(2)}, u32[]{:S(2)}) async-start(f32[2,4096,128]{2,1,0:T(8,128)} %bitcast.21), calls=%async_computation | async-start | bytes 8388608 | tf_op jit(solution)/shard_map/all_to_all | solution.py:21
  12.9 72.2 %all-gather.8.cloned.1.call-start = ((), (), s32[]{:S(2)}) async-start(), calls=%async_computation.2 | async-start | bytes 2359296 | tf_op jit(solution)/shard_map/all_gather | solution.py:22
  56.4 317.6 %all-gather.10.cloned.1.call-start = ((), (), s32[]{:S(2)}) async-start(), calls=%async_computation.3 | async-start | bytes 20971520 | tf_op jit(solution)/shard_map/all_gather | solution.py:24
  75.8 473.8 %all-gather.12.cloned.1.call-start = ((), (), s32[]{:S(2)}) async-start(), calls=%async_computation.4 | async-start | bytes 18874368 | tf_op jit(solution)/shard_map/all_gather | solution.py:34
  549.6 11.1 %copy-start.1 = (f32[1024,512]{1,0:T(8,128)S(1)}, f32[1024,512]{1,0:T(8,128)}, u32[]{:S(2)}) copy-start(f32[1024,512]{1,0:T(8,128)} %param.4) | copy-start | bytes 6291460
Sparse Core Ops, SparseCore 0:
  9.2 34.7 all-gather.5
  56.6 28.4 all-gather.7
  86.6 287.3 all-gather.9
  398.8 150.6 all-gather.11
